TPU v7x, 32 devices: a whole 2x2x4 slice. The times are simulated.
32 devices in a mesh: gx: 4 (over y, core), gy: 2 (over x), gz: 4 (over z).
Axes of the slice: x: 2, y: 2, z: 4, core: 2. Of those that a mesh axis runs over, the one named last changes fastest.
Arguments:
- noisy_image: float32 [32, 64, 512], P('gz', 'gy', 'gx'), may hold values from -6 to 6
- fidelity: float32 [32, 64, 512], P('gz', 'gy', 'gx'), may hold values from 0.5 to 8
- primal_u: float32 [32, 64, 512], P('gz', 'gy', 'gx'), may hold values from -6 to 6
- primal_v: float32 [3, 32, 64, 512], P(None, 'gz', 'gy', 'gx'), may hold values from -2 to 2
- dual_p: float32 [3, 32, 64, 512], P(None, 'gz', 'gy', 'gx'), may hold values from -2.5 to 2.5
- dual_q: float32 [6, 32, 64, 512], P(None, 'gz', 'gy', 'gx'), may hold values from -2.5 to 2.5
Outputs:
- denoised: float32 [32, 64, 512], P('gz', 'gy', 'gx')
- vector_field: float32 [3, 32, 64, 512], P(None, 'gz', 'gy', 'gx')
- grad_dual: float32 [3, 32, 64, 512], P(None, 'gz', 'gy', 'gx')
- sym_dual: float32 [6, 32, 64, 512], P(None, 'gz', 'gy', 'gx')
All inputs are finite; a program needn't handle non-finite values.
Results may differ from a plain program's by a relative error of at most 0.0001.
Values sent between devices are 32-bit elements; how exact they have to be, the bound alone decides.
A program may use at most 64 MiB of HBM per device.

v0:
```python
import jax
import jax.numpy as jnp
from jax import lax
from jax.sharding import PartitionSpec as P

ITERS = 3


first_alpha = 0.5
second_alpha = 1.0
dual_step = 0.2
primal_step = 0.2
index_pairs = ((0, 0), (1, 1), (2, 2), (0, 1), (0, 2), (1, 2))


def passed_along(shard, axis, by):
    devices = lax.axis_size(axis)
    pairs = [(i, i + by) for i in range(devices) if 0 <= i + by < devices]
    return lax.ppermute(shard, axis, pairs)


def pair_index(left_axis, right_axis):
    for position, entry_pair in enumerate(index_pairs):
        if entry_pair == (left_axis, right_axis) or entry_pair == (right_axis, left_axis):
            return position
    return 0


def first_layer(values, axis_dim):
    return lax.slice_in_dim(values, 0, 1, axis=axis_dim)


def last_layer(values, axis_dim):
    extent = values.shape[axis_dim]
    return lax.slice_in_dim(values, extent - 1, extent, axis=axis_dim)


def following(values, border, axis_dim):
    extent = values.shape[axis_dim]
    return jnp.concatenate(
        [lax.slice_in_dim(values, 1, extent, axis=axis_dim), border], axis=axis_dim
    )


def preceding(values, border, axis_dim):
    extent = values.shape[axis_dim]
    return jnp.concatenate(
        [border, lax.slice_in_dim(values, 0, extent - 1, axis=axis_dim)], axis=axis_dim
    )


def edge_masks(extents, margin):
    device_places = (lax.axis_index("gx"), lax.axis_index("gy"), lax.axis_index("gz"))
    group_sizes = (lax.axis_size("gx"), lax.axis_size("gy"), lax.axis_size("gz"))
    lower_masks = []
    upper_masks = []
    inside = jnp.ones((1, 1, 1, 1), jnp.float32)
    for component in range(3):
        extent = extents[2 - component]
        places = (
            device_places[component] * extent - margin + lax.iota(jnp.int32, extent + 2 * margin)
        )
        full_extent = group_sizes[component] * extent
        shape_list = [1, 1, 1, 1]
        shape_list[3 - component] = extent + 2 * margin
        upper_masks.append((places < full_extent - 1).astype(jnp.float32).reshape(shape_list))
        lower_masks.append((places > 0).astype(jnp.float32).reshape(shape_list))
        within = jnp.logical_and(places >= 0, places < full_extent)
        inside = inside * within.astype(jnp.float32).reshape(shape_list)
    return (lower_masks, upper_masks, inside)


def q_rows(stacked, column):
    return jnp.stack([stacked[pair_index(row_axis, column)] for row_axis in range(3)], axis=0)


def project(stacked, weights, bound):
    magnitude = jnp.sqrt(jnp.sum(weights * stacked * stacked, axis=0, keepdims=True))
    return stacked / jnp.maximum(1.0, magnitude / bound)


def dual_update(bar_u, bar_v, grad_dual, sym_dual, next_u, prev_v, lower_masks, upper_masks):
    grads = jnp.concatenate(
        [upper_masks[component] * (next_u[component] - bar_u) for component in range(3)], axis=0
    )
    trial_p = grad_dual + dual_step * (grads - bar_v)
    new_p = project(trial_p, jnp.ones((3, 1, 1, 1), jnp.float32), first_alpha)
    derivs = [lower_masks[component] * (bar_v - prev_v[component]) for component in range(3)]
    sym_parts = []
    for left_axis, right_axis in index_pairs:
        sym_parts.append(0.5 * (derivs[right_axis][left_axis] + derivs[left_axis][right_axis]))
    trial_q = sym_dual + dual_step * jnp.stack(sym_parts, axis=0)
    weights = jnp.array([1.0, 1.0, 1.0, 2.0, 2.0, 2.0], jnp.float32).reshape((6, 1, 1, 1))
    new_q = project(trial_q, weights, second_alpha)
    return (new_p, new_q)


def primal_update(
    image_u,
    vector_v,
    grad_dual,
    sym_dual,
    noisy,
    weight_map,
    prev_p,
    next_q,
    lower_masks,
    upper_masks,
):
    divergence = jnp.zeros_like(image_u)
    second_div = jnp.zeros_like(vector_v)
    for component in range(3):
        divergence = (
            divergence
            + upper_masks[component] * grad_dual[component : component + 1]
            - prev_p[component]
        )
        second_div = (
            second_div + next_q[component] - lower_masks[component] * q_rows(sym_dual, component)
        )
    new_u = (image_u + primal_step * divergence + primal_step * weight_map * noisy) / (
        1.0 + primal_step * weight_map
    )
    new_v = vector_v + primal_step * (grad_dual + second_div)
    return (new_u, new_v)


def per_device(noisy_image, fidelity, primal_u, primal_v, dual_p, dual_q):
    noisy = noisy_image[None]
    weight_map = fidelity[None]
    image_u = primal_u[None]
    vector_v = primal_v
    grad_dual = dual_p
    sym_dual = dual_q
    lower_masks, upper_masks, unused_inside = edge_masks(noisy_image.shape, 0)
    bar_u = image_u
    bar_v = vector_v
    for step_index in range(ITERS):
        next_u = [
            following(bar_u, passed_along(first_layer(bar_u, 3), "gx", -1), 3),
            following(bar_u, passed_along(first_layer(bar_u, 2), "gy", -1), 2),
            following(bar_u, passed_along(first_layer(bar_u, 1), "gz", -1), 1),
        ]
        prev_v = [
            preceding(bar_v, passed_along(last_layer(bar_v, 3), "gx", 1), 3),
            preceding(bar_v, passed_along(last_layer(bar_v, 2), "gy", 1), 2),
            preceding(bar_v, passed_along(last_layer(bar_v, 1), "gz", 1), 1),
        ]
        grad_dual, sym_dual = dual_update(
            bar_u, bar_v, grad_dual, sym_dual, next_u, prev_v, lower_masks, upper_masks
        )
        grad_x = grad_dual[0:1]
        grad_y = grad_dual[1:2]
        grad_z = grad_dual[2:3]
        prev_p = [
            preceding(grad_x, passed_along(last_layer(grad_x, 3), "gx", 1), 3),
            preceding(grad_y, passed_along(last_layer(grad_y, 2), "gy", 1), 2),
            preceding(grad_z, passed_along(last_layer(grad_z, 1), "gz", 1), 1),
        ]
        rows_x = q_rows(sym_dual, 0)
        rows_y = q_rows(sym_dual, 1)
        rows_z = q_rows(sym_dual, 2)
        next_q = [
            following(rows_x, passed_along(first_layer(rows_x, 3), "gx", -1), 3),
            following(rows_y, passed_along(first_layer(rows_y, 2), "gy", -1), 2),
            following(rows_z, passed_along(first_layer(rows_z, 1), "gz", -1), 1),
        ]
        new_u, new_v = primal_update(
            image_u,
            vector_v,
            grad_dual,
            sym_dual,
            noisy,
            weight_map,
            prev_p,
            next_q,
            lower_masks,
            upper_masks,
        )
        bar_u = 2.0 * new_u - image_u
        bar_v = 2.0 * new_v - vector_v
        image_u = new_u
        vector_v = new_v
    return (image_u[0], vector_v, grad_dual, sym_dual)


def solution(mesh):
    in_specs = (
        P("gz", "gy", "gx"),
        P("gz", "gy", "gx"),
        P("gz", "gy", "gx"),
        P(None, "gz", "gy", "gx"),
        P(None, "gz", "gy", "gx"),
        P(None, "gz", "gy", "gx"),
    )
    out_specs = (
        P("gz", "gy", "gx"),
        P(None, "gz", "gy", "gx"),
        P(None, "gz", "gy", "gx"),
        P(None, "gz", "gy", "gx"),
    )
    return jax.shard_map(
        per_device, mesh=mesh, in_specs=in_specs, out_specs=out_specs, check_vma=False
    )
```

profile of v0, /device:TPU:0, one launch (start us, length us, event | category | flops | bytes accessed | tf_op | source)
XLA Modules:
  0.0 155.0 jit_solution(12084420073467371968)
XLA Ops:
  3.7 4.9 %collective-permute-start.10 = (f32[3,8,1,128]{3,1,2,0:T(8,128)S(1)}, f32[3,8,1,128]{3,1,2,0:T(8,128)S(1)}, u32[]{:S(2)}, u32[]{:S(2)}) collective-permute-start(f32[3,8,1,128]{3,1,2,0:T(8,128)S(1)} %bitcast.80), channel_id=1, source_target_pairs={{0,4},{1,5},{2,6},{3,7},{8,12},{9,13},{10,14},{11,15},{16,20},{17,... | collective-permute-start | bytes 36872 | tf_op jit(solution)/shard_map/ppermute | solution.py:19
  11.4 5.2 %collective-permute-start.11 = (f32[3,1,32,128]{3,2,1,0:T(8,128)S(1)}, f32[3,1,32,128]{3,2,1,0:T(8,128)S(1)}, u32[]{:S(2)}, u32[]{:S(2)}) collective-permute-start(f32[3,1,32,128]{3,2,1,0:T(8,128)S(1)} %slice.489), channel_id=1, source_target_pairs={{0,1},{1,2},{2,3},{4,5},{5,6},{6,7},{8,9},{9,10},{10,11},{12,13},{... | collective-permute-start | bytes 147464 | tf_op jit(solution)/shard_map/ppermute | solution.py:19
  16.6 1.3 collective-permute-start
  19.9 5.3 %collective-permute-start.9 = (f32[3,8,32,1]{3,2,1,0:T(8,128)S(1)}, f32[3,8,32,1]{3,2,1,0:T(8,128)S(1)}, u32[]{:S(2)}, u32[]{:S(2)}) collective-permute-start(f32[3,8,32,1]{3,2,1,0:T(8,128)S(1)} %slice.483), channel_id=1, source_target_pairs={{0,8},{8,16},{16,24},{1,9},{9,17},{17,25},{2,10},{10,18},{18,26},{... | collective-permute-start | bytes 9224 | tf_op jit(solution)/shard_map/ppermute | solution.py:19
  30.5 3.5 %collective-permute-start.5 = (f32[1,1,32,128]{3,2,1,0:T(8,128)S(1)}, f32[1,1,32,128]{3,2,1,0:T(8,128)S(1)}, u32[]{:S(2)}, u32[]{:S(2)}) collective-permute-start(f32[1,1,32,128]{3,2,1,0:T(8,128)S(1)} %slice.604), channel_id=1, source_target_pairs={{0,1},{1,2},{2,3},{4,5},{5,6},{6,7},{8,9},{9,10},{10,11},{12,13},{... | collective-permute-start | bytes 49160 | tf_op jit(solution)/shard_map/ppermute | solution.py:19
  34.0 5.0 %collective-permute-start.3 = (f32[1,8,32,1]{3,2,1,0:T(8,128)S(1)}, f32[1,8,32,1]{3,2,1,0:T(8,128)S(1)}, u32[]{:S(2)}, u32[]{:S(2)}) collective-permute-start(f32[1,8,32,1]{3,2,1,0:T(8,128)S(1)} %slice.598), channel_id=1, source_target_pairs={{0,8},{8,16},{16,24},{1,9},{9,17},{17,25},{2,10},{10,18},{18,26},{... | collective-permute-start | bytes 3080 | tf_op jit(solution)/shard_map/ppermute | solution.py:19
  40.3 1.3 collective-permute-start.7
  41.6 1.3 collective-permute-start.8
  42.9 1.3 collective-permute-start.6
  44.3 1.3 collective-permute-start.14
  45.6 1.3 collective-permute-start.13
  47.1 2.3 %collective-permute-done.6 = f32[1,8,32,1]{3,2,1,0:T(8,128)S(1)} collective-permute-done((f32[1,8,32,1]{3,2,1,0:T(8,128)S(1)}, f32[1,8,32,1]{3,2,1,0:T(8,128)S(1)}, u32[]{:S(2)}, u32[]{:S(2)}) %collective-permute-start.6) | collective-permute-done | bytes 1056 | tf_op jit(solution)/shard_map/ppermute | solution.py:19
  50.8 5.9 %collective-permute-done.12 = f32[3,8,32,1]{3,2,1,0:T(8,128)S(1)} collective-permute-done((f32[3,8,32,1]{3,2,1,0:T(8,128)S(1)}, f32[3,8,32,1]{3,2,1,0:T(8,128)S(1)}, u32[]{:S(2)}, u32[]{:S(2)}) %collective-permute-start.12) | collective-permute-done | bytes 3104 | tf_op jit(solution)/shard_map/ppermute | solution.py:19
  57.4 4.5 %collective-permute-start.22 = (f32[3,8,1,128]{3,1,2,0:T(8,128)S(1)}, f32[3,8,1,128]{3,1,2,0:T(8,128)S(1)}, u32[]{:S(2)}, u32[]{:S(2)}) collective-permute-start(f32[3,8,1,128]{3,1,2,0:T(8,128)S(1)} %bitcast.83), channel_id=1, source_target_pairs={{0,4},{1,5},{2,6},{3,7},{8,12},{9,13},{10,14},{11,15},{16,20},{17,... | collective-permute-start | bytes 36872 | tf_op jit(solution)/shard_map/ppermute | solution.py:19
  61.9 4.5 %collective-permute-start.23 = (f32[3,1,32,128]{3,2,1,0:T(8,128)S(1)}, f32[3,1,32,128]{3,2,1,0:T(8,128)S(1)}, u32[]{:S(2)}, u32[]{:S(2)}) collective-permute-start(f32[3,1,32,128]{3,2,1,0:T(8,128)S(1)} %slice.659), channel_id=1, source_target_pairs={{0,1},{1,2},{2,3},{4,5},{5,6},{6,7},{8,9},{9,10},{10,11},{12,13},{... | collective-permute-start | bytes 147464 | tf_op jit(solution)/shard_map/ppermute | solution.py:19
  66.5 7.3 %collective-permute-start.21 = (f32[3,8,32,1]{3,2,1,0:T(8,128)S(1)}, f32[3,8,32,1]{3,2,1,0:T(8,128)S(1)}, u32[]{:S(2)}, u32[]{:S(2)}) collective-permute-start(f32[3,8,32,1]{3,2,1,0:T(8,128)S(1)} %slice.653), channel_id=1, source_target_pairs={{0,8},{8,16},{16,24},{1,9},{9,17},{17,25},{2,10},{10,18},{18,26},{... | collective-permute-start | bytes 9224 | tf_op jit(solution)/shard_map/ppermute | solution.py:19
  76.6 1.6 %collective-permute-start.16 = (f32[1,8,1,128]{3,2,1,0:T(1,128)S(1)}, f32[1,8,1,128]{3,2,1,0:T(1,128)S(1)}, u32[]{:S(2)}, u32[]{:S(2)}) collective-permute-start(f32[1,8,1,128]{3,2,1,0:T(1,128)S(1)} %slice.642), channel_id=1, source_target_pairs={{0,4},{1,5},{2,6},{3,7},{8,12},{9,13},{10,14},{11,15},{16,20},{17,... | collective-permute-start | bytes 12296 | tf_op jit(solution)/shard_map/ppermute | solution.py:19
  78.2 3.5 %collective-permute-start.17 = (f32[1,1,32,128]{3,2,1,0:T(8,128)S(1)}, f32[1,1,32,128]{3,2,1,0:T(8,128)S(1)}, u32[]{:S(2)}, u32[]{:S(2)}) collective-permute-start(f32[1,1,32,128]{3,2,1,0:T(8,128)S(1)} %slice.645), channel_id=1, source_target_pairs={{0,1},{1,2},{2,3},{4,5},{5,6},{6,7},{8,9},{9,10},{10,11},{12,13},{... | collective-permute-start | bytes 49160 | tf_op jit(solution)/shard_map/ppermute | solution.py:19
  81.7 5.1 %collective-permute-start.15 = (f32[1,8,32,1]{3,2,1,0:T(8,128)S(1)}, f32[1,8,32,1]{3,2,1,0:T(8,128)S(1)}, u32[]{:S(2)}, u32[]{:S(2)}) collective-permute-start(f32[1,8,32,1]{3,2,1,0:T(8,128)S(1)} %slice.639), channel_id=1, source_target_pairs={{0,8},{8,16},{16,24},{1,9},{9,17},{17,25},{2,10},{10,18},{18,26},{... | collective-permute-start | bytes 3080 | tf_op jit(solution)/shard_map/ppermute | solution.py:19
  88.0 1.3 collective-permute-start.19
  92.0 1.3 collective-permute-start.26
  93.3 1.3 collective-permute-start.25
  94.7 2.4 %collective-permute-done.18 = f32[1,8,32,1]{3,2,1,0:T(8,128)S(1)} collective-permute-done((f32[1,8,32,1]{3,2,1,0:T(8,128)S(1)}, f32[1,8,32,1]{3,2,1,0:T(8,128)S(1)}, u32[]{:S(2)}, u32[]{:S(2)}) %collective-permute-start.18) | collective-permute-done | bytes 1056 | tf_op jit(solution)/shard_map/ppermute | solution.py:19
  98.5 5.9 %collective-permute-done.24 = f32[3,8,32,1]{3,2,1,0:T(8,128)S(1)} collective-permute-done((f32[3,8,32,1]{3,2,1,0:T(8,128)S(1)}, f32[3,8,32,1]{3,2,1,0:T(8,128)S(1)}, u32[]{:S(2)}, u32[]{:S(2)}) %collective-permute-start.24) | collective-permute-done | bytes 3104 | tf_op jit(solution)/shard_map/ppermute | solution.py:19
  105.2 4.5 %collective-permute-start.31 = (f32[3,8,1,128]{3,1,2,0:T(8,128)S(1)}, f32[3,8,1,128]{3,1,2,0:T(8,128)S(1)}, u32[]{:S(2)}, u32[]{:S(2)}) collective-permute-start(f32[3,8,1,128]{3,1,2,0:T(8,128)S(1)} %bitcast.84), channel_id=1, source_target_pairs={{0,4},{1,5},{2,6},{3,7},{8,12},{9,13},{10,14},{11,15},{16,20},{17,... | collective-permute-start | bytes 36872 | tf_op jit(solution)/shard_map/ppermute | solution.py:19
  109.7 4.5 %collective-permute-start.32 = (f32[3,1,32,128]{3,2,1,0:T(8,128)S(1)}, f32[3,1,32,128]{3,2,1,0:T(8,128)S(1)}, u32[]{:S(2)}, u32[]{:S(2)}) collective-permute-start(f32[3,1,32,128]{3,2,1,0:T(8,128)S(1)} %slice.700), channel_id=1, source_target_pairs={{0,1},{1,2},{2,3},{4,5},{5,6},{6,7},{8,9},{9,10},{10,11},{12,13},{... | collective-permute-start | bytes 147464 | tf_op jit(solution)/shard_map/ppermute | solution.py:19
  114.3 7.3 %collective-permute-start.30 = (f32[3,8,32,1]{3,2,1,0:T(8,128)S(1)}, f32[3,8,32,1]{3,2,1,0:T(8,128)S(1)}, u32[]{:S(2)}, u32[]{:S(2)}) collective-permute-start(f32[3,8,32,1]{3,2,1,0:T(8,128)S(1)} %slice.694), channel_id=1, source_target_pairs={{0,8},{8,16},{16,24},{1,9},{9,17},{17,25},{2,10},{10,18},{18,26},{... | collective-permute-start | bytes 9224 | tf_op jit(solution)/shard_map/ppermute | solution.py:19
  129.0 5.5 %collective-permute-done.33 = f32[3,8,32,1]{3,2,1,0:T(8,128)S(1)} collective-permute-done((f32[3,8,32,1]{3,2,1,0:T(8,128)S(1)}, f32[3,8,32,1]{3,2,1,0:T(8,128)S(1)}, u32[]{:S(2)}, u32[]{:S(2)}) %collective-permute-start.33) | collective-permute-done | bytes 3104 | tf_op jit(solution)/shard_map/ppermute | solution.py:19
  134.6 1.3 fusion.13
  135.9 4.3 %collective-permute-start.29 = (f32[1,1,32,128]{3,2,1,0:T(8,128)S(1)}, f32[1,1,32,128]{3,2,1,0:T(8,128)S(1)}, u32[]{:S(2)}, u32[]{:S(2)}) collective-permute-start(f32[1,1,32,128]{3,2,1,0:T(8,128)S(1)} %slice.692), channel_id=1, source_target_pairs={{0,1},{1,2},{2,3},{4,5},{5,6},{6,7},{8,9},{9,10},{10,11},{12,13},{... | collective-permute-start | bytes 49160 | tf_op jit(solution)/shard_map/ppermute | solution.py:19
  140.1 4.3 %collective-permute-start.28 = (f32[1,8,1,128]{3,2,1,0:T(1,128)S(1)}, f32[1,8,1,128]{3,2,1,0:T(1,128)S(1)}, u32[]{:S(2)}, u32[]{:S(2)}) collective-permute-start(f32[1,8,1,128]{3,2,1,0:T(1,128)S(1)} %slice.689), channel_id=1, source_target_pairs={{0,4},{1,5},{2,6},{3,7},{8,12},{9,13},{10,14},{11,15},{16,20},{17,... | collective-permute-start | bytes 12296 | tf_op jit(solution)/shard_map/ppermute | solution.py:19
  144.5 8.6 %collective-permute-start.27 = (f32[1,8,32,1]{3,2,1,0:T(8,128)S(1)}, f32[1,8,32,1]{3,2,1,0:T(8,128)S(1)}, u32[]{:S(2)}, u32[]{:S(2)}) collective-permute-start(f32[1,8,32,1]{3,2,1,0:T(8,128)S(1)} %slice.686), channel_id=1, source_target_pairs={{0,8},{8,16},{16,24},{1,9},{9,17},{17,25},{2,10},{10,18},{18,26},{... | collective-permute-start | bytes 3080 | tf_op jit(solution)/shard_map/ppermute | solution.py:19
  (179 shorter events, 34.0 us)
Async XLA Ops:
  1.5 23.7 %collective-permute-start.1 = (f32[1,8,1,128]{3,2,1,0:T(1,128)S(1)}, f32[1,8,1,128]{3,2,1,0:T(1,128)S(1)}, u32[]{:S(2)}, u32[]{:S(2)}) collective-permute-start(f32[1,8,1,128]{3,2,1,0:T(1,128)S(1)} %slice.594), channel_id=1, source_target_pairs={{4,0},{5,1},{6,2},{7,3},{12,8},{13,9},{14,10},{15,11},{20,16},{21,... | collective-permute-start | bytes 12296 | tf_op jit(solution)/shard_map/ppermute | solution.py:19
  3.7 22.8 %collective-permute-start.10 = (f32[3,8,1,128]{3,1,2,0:T(8,128)S(1)}, f32[3,8,1,128]{3,1,2,0:T(8,128)S(1)}, u32[]{:S(2)}, u32[]{:S(2)}) collective-permute-start(f32[3,8,1,128]{3,1,2,0:T(8,128)S(1)} %bitcast.80), channel_id=1, source_target_pairs={{0,4},{1,5},{2,6},{3,7},{8,12},{9,13},{10,14},{11,15},{16,20},{17,... | collective-permute-start | bytes 36872 | tf_op jit(solution)/shard_map/ppermute | solution.py:19
  9.3 15.9 %collective-permute-start.2 = (f32[1,1,32,128]{3,2,1,0:T(8,128)S(1)}, f32[1,1,32,128]{3,2,1,0:T(8,128)S(1)}, u32[]{:S(2)}, u32[]{:S(2)}) collective-permute-start(f32[1,1,32,128]{3,2,1,0:T(8,128)S(1)} %slice.596), channel_id=1, source_target_pairs={{1,0},{2,1},{3,2},{5,4},{6,5},{7,6},{9,8},{10,9},{11,10},{13,12},{... | collective-permute-start | bytes 49160 | tf_op jit(solution)/shard_map/ppermute | solution.py:19
  11.4 15.1 %collective-permute-start.11 = (f32[3,1,32,128]{3,2,1,0:T(8,128)S(1)}, f32[3,1,32,128]{3,2,1,0:T(8,128)S(1)}, u32[]{:S(2)}, u32[]{:S(2)}) collective-permute-start(f32[3,1,32,128]{3,2,1,0:T(8,128)S(1)} %slice.489), channel_id=1, source_target_pairs={{0,1},{1,2},{2,3},{4,5},{5,6},{6,7},{8,9},{9,10},{10,11},{12,13},{... | collective-permute-start | bytes 147464 | tf_op jit(solution)/shard_map/ppermute | solution.py:19
  19.9 6.6 %collective-permute-start.9 = (f32[3,8,32,1]{3,2,1,0:T(8,128)S(1)}, f32[3,8,32,1]{3,2,1,0:T(8,128)S(1)}, u32[]{:S(2)}, u32[]{:S(2)}) collective-permute-start(f32[3,8,32,1]{3,2,1,0:T(8,128)S(1)} %slice.483), channel_id=1, source_target_pairs={{0,8},{8,16},{16,24},{1,9},{9,17},{17,25},{2,10},{10,18},{18,26},{... | collective-permute-start | bytes 9224 | tf_op jit(solution)/shard_map/ppermute | solution.py:19
  29.2 10.8 %collective-permute-start.4 = (f32[1,8,1,128]{3,2,1,0:T(1,128)S(1)}, f32[1,8,1,128]{3,2,1,0:T(1,128)S(1)}, u32[]{:S(2)}, u32[]{:S(2)}) collective-permute-start(f32[1,8,1,128]{3,2,1,0:T(1,128)S(1)} %slice.601), channel_id=1, source_target_pairs={{0,4},{1,5},{2,6},{3,7},{8,12},{9,13},{10,14},{11,15},{16,20},{17,... | collective-permute-start | bytes 12296 | tf_op jit(solution)/shard_map/ppermute | solution.py:19
  30.5 9.5 %collective-permute-start.5 = (f32[1,1,32,128]{3,2,1,0:T(8,128)S(1)}, f32[1,1,32,128]{3,2,1,0:T(8,128)S(1)}, u32[]{:S(2)}, u32[]{:S(2)}) collective-permute-start(f32[1,1,32,128]{3,2,1,0:T(8,128)S(1)} %slice.604), channel_id=1, source_target_pairs={{0,1},{1,2},{2,3},{4,5},{5,6},{6,7},{8,9},{9,10},{10,11},{12,13},{... | collective-permute-start | bytes 49160 | tf_op jit(solution)/shard_map/ppermute | solution.py:19
  40.3 10.3 %collective-permute-start.7 = (f32[1,8,1,128]{3,2,1,0:T(1,128)S(1)}, f32[1,8,1,128]{3,2,1,0:T(1,128)S(1)}, u32[]{:S(2)}, u32[]{:S(2)}) collective-permute-start(f32[1,8,1,128]{3,2,1,0:T(1,128)S(1)} %slice.609), channel_id=1, source_target_pairs={{4,0},{5,1},{6,2},{7,3},{12,8},{13,9},{14,10},{15,11},{20,16},{21,... | collective-permute-start | bytes 12296 | tf_op jit(solution)/shard_map/ppermute | solution.py:19
  41.6 9.0 %collective-permute-start.8 = (f32[1,1,32,128]{3,2,1,0:T(8,128)S(1)}, f32[1,1,32,128]{3,2,1,0:T(8,128)S(1)}, u32[]{:S(2)}, u32[]{:S(2)}) collective-permute-start(f32[1,1,32,128]{3,2,1,0:T(8,128)S(1)} %slice.611), channel_id=1, source_target_pairs={{1,0},{2,1},{3,2},{5,4},{6,5},{7,6},{9,8},{10,9},{11,10},{13,12},{... | collective-permute-start | bytes 49160 | tf_op jit(solution)/shard_map/ppermute | solution.py:19
  44.3 12.4 %collective-permute-start.14 = (f32[3,1,32,128]{3,2,1,0:T(8,128)S(1)}, f32[3,1,32,128]{3,2,1,0:T(8,128)S(1)}, u32[]{:S(2)}, u32[]{:S(2)}) collective-permute-start(f32[3,1,32,128]{3,2,1,0:T(8,128)S(1)} %fusion.135), channel_id=1, source_target_pairs={{1,0},{2,1},{3,2},{5,4},{6,5},{7,6},{9,8},{10,9},{11,10},{13,12},{... | collective-permute-start | bytes 147464 | tf_op jit(solution)/shard_map/ppermute | solution.py:19
  45.6 11.1 %collective-permute-start.13 = (f32[3,8,1,128]{3,1,2,0:T(8,128)S(1)}, f32[3,8,1,128]{3,1,2,0:T(8,128)S(1)}, u32[]{:S(2)}, u32[]{:S(2)}) collective-permute-start(f32[3,8,1,128]{3,1,2,0:T(8,128)S(1)} %bitcast.81), channel_id=1, source_target_pairs={{4,0},{5,1},{6,2},{7,3},{12,8},{13,9},{14,10},{15,11},{20,16},{21,... | collective-permute-start | bytes 36872 | tf_op jit(solution)/shard_map/ppermute | solution.py:19
  49.3 7.4 %collective-permute-start.12 = (f32[3,8,32,1]{3,2,1,0:T(8,128)S(1)}, f32[3,8,32,1]{3,2,1,0:T(8,128)S(1)}, u32[]{:S(2)}, u32[]{:S(2)}) collective-permute-start(f32[3,8,32,1]{3,2,1,0:T(8,128)S(1)} %fusion.8), channel_id=1, source_target_pairs={{8,0},{16,8},{24,16},{9,1},{17,9},{25,17},{10,2},{18,10},{26,18},{... | collective-permute-start | bytes 9224 | tf_op jit(solution)/shard_map/ppermute | solution.py:19
  57.4 17.8 %collective-permute-start.22 = (f32[3,8,1,128]{3,1,2,0:T(8,128)S(1)}, f32[3,8,1,128]{3,1,2,0:T(8,128)S(1)}, u32[]{:S(2)}, u32[]{:S(2)}) collective-permute-start(f32[3,8,1,128]{3,1,2,0:T(8,128)S(1)} %bitcast.83), channel_id=1, source_target_pairs={{0,4},{1,5},{2,6},{3,7},{8,12},{9,13},{10,14},{11,15},{16,20},{17,... | collective-permute-start | bytes 36872 | tf_op jit(solution)/shard_map/ppermute | solution.py:19
  61.9 13.2 %collective-permute-start.23 = (f32[3,1,32,128]{3,2,1,0:T(8,128)S(1)}, f32[3,1,32,128]{3,2,1,0:T(8,128)S(1)}, u32[]{:S(2)}, u32[]{:S(2)}) collective-permute-start(f32[3,1,32,128]{3,2,1,0:T(8,128)S(1)} %slice.659), channel_id=1, source_target_pairs={{0,1},{1,2},{2,3},{4,5},{5,6},{6,7},{8,9},{9,10},{10,11},{12,13},{... | collective-permute-start | bytes 147464 | tf_op jit(solution)/shard_map/ppermute | solution.py:19
  66.5 8.7 %collective-permute-start.21 = (f32[3,8,32,1]{3,2,1,0:T(8,128)S(1)}, f32[3,8,32,1]{3,2,1,0:T(8,128)S(1)}, u32[]{:S(2)}, u32[]{:S(2)}) collective-permute-start(f32[3,8,32,1]{3,2,1,0:T(8,128)S(1)} %slice.653), channel_id=1, source_target_pairs={{0,8},{8,16},{16,24},{1,9},{9,17},{17,25},{2,10},{10,18},{18,26},{... | collective-permute-start | bytes 9224 | tf_op jit(solution)/shard_map/ppermute | solution.py:19
  76.6 11.2 %collective-permute-start.16 = (f32[1,8,1,128]{3,2,1,0:T(1,128)S(1)}, f32[1,8,1,128]{3,2,1,0:T(1,128)S(1)}, u32[]{:S(2)}, u32[]{:S(2)}) collective-permute-start(f32[1,8,1,128]{3,2,1,0:T(1,128)S(1)} %slice.642), channel_id=1, source_target_pairs={{0,4},{1,5},{2,6},{3,7},{8,12},{9,13},{10,14},{11,15},{16,20},{17,... | collective-permute-start | bytes 12296 | tf_op jit(solution)/shard_map/ppermute | solution.py:19
  78.2 9.6 %collective-permute-start.17 = (f32[1,1,32,128]{3,2,1,0:T(8,128)S(1)}, f32[1,1,32,128]{3,2,1,0:T(8,128)S(1)}, u32[]{:S(2)}, u32[]{:S(2)}) collective-permute-start(f32[1,1,32,128]{3,2,1,0:T(8,128)S(1)} %slice.645), channel_id=1, source_target_pairs={{0,1},{1,2},{2,3},{4,5},{5,6},{6,7},{8,9},{9,10},{10,11},{12,13},{... | collective-permute-start | bytes 49160 | tf_op jit(solution)/shard_map/ppermute | solution.py:19
  88.0 10.4 %collective-permute-start.19 = (f32[1,8,1,128]{3,2,1,0:T(1,128)S(1)}, f32[1,8,1,128]{3,2,1,0:T(1,128)S(1)}, u32[]{:S(2)}, u32[]{:S(2)}) collective-permute-start(f32[1,8,1,128]{3,2,1,0:T(1,128)S(1)} %slice.650), channel_id=1, source_target_pairs={{4,0},{5,1},{6,2},{7,3},{12,8},{13,9},{14,10},{15,11},{20,16},{21,... | collective-permute-start | bytes 12296 | tf_op jit(solution)/shard_map/ppermute | solution.py:19
  89.3 9.1 %collective-permute-start.20 = (f32[1,1,32,128]{3,2,1,0:T(8,128)S(1)}, f32[1,1,32,128]{3,2,1,0:T(8,128)S(1)}, u32[]{:S(2)}, u32[]{:S(2)}) collective-permute-start(f32[1,1,32,128]{3,2,1,0:T(8,128)S(1)} %slice.652), channel_id=1, source_target_pairs={{1,0},{2,1},{3,2},{5,4},{6,5},{7,6},{9,8},{10,9},{11,10},{13,12},{... | collective-permute-start | bytes 49160 | tf_op jit(solution)/shard_map/ppermute | solution.py:19
  90.6 6.5 %collective-permute-start.18 = (f32[1,8,32,1]{3,2,1,0:T(8,128)S(1)}, f32[1,8,32,1]{3,2,1,0:T(8,128)S(1)}, u32[]{:S(2)}, u32[]{:S(2)}) collective-permute-start(f32[1,8,32,1]{3,2,1,0:T(8,128)S(1)} %bitcast.72), channel_id=1, source_target_pairs={{8,0},{16,8},{24,16},{9,1},{17,9},{25,17},{10,2},{18,10},{26,18},{... | collective-permute-start | bytes 3080 | tf_op jit(solution)/shard_map/ppermute | solution.py:19
  92.0 12.5 %collective-permute-start.26 = (f32[3,1,32,128]{3,2,1,0:T(8,128)S(1)}, f32[3,1,32,128]{3,2,1,0:T(8,128)S(1)}, u32[]{:S(2)}, u32[]{:S(2)}) collective-permute-start(f32[3,1,32,128]{3,2,1,0:T(8,128)S(1)} %fusion.134), channel_id=1, source_target_pairs={{1,0},{2,1},{3,2},{5,4},{6,5},{7,6},{9,8},{10,9},{11,10},{13,12},{... | collective-permute-start | bytes 147464 | tf_op jit(solution)/shard_map/ppermute | solution.py:19
  93.3 11.2 %collective-permute-start.25 = (f32[3,8,1,128]{3,1,2,0:T(8,128)S(1)}, f32[3,8,1,128]{3,1,2,0:T(8,128)S(1)}, u32[]{:S(2)}, u32[]{:S(2)}) collective-permute-start(f32[3,8,1,128]{3,1,2,0:T(8,128)S(1)} %bitcast.82), channel_id=1, source_target_pairs={{4,0},{5,1},{6,2},{7,3},{12,8},{13,9},{14,10},{15,11},{20,16},{21,... | collective-permute-start | bytes 36872 | tf_op jit(solution)/shard_map/ppermute | solution.py:19
  97.1 7.4 %collective-permute-start.24 = (f32[3,8,32,1]{3,2,1,0:T(8,128)S(1)}, f32[3,8,32,1]{3,2,1,0:T(8,128)S(1)}, u32[]{:S(2)}, u32[]{:S(2)}) collective-permute-start(f32[3,8,32,1]{3,2,1,0:T(8,128)S(1)} %fusion.6), channel_id=1, source_target_pairs={{8,0},{16,8},{24,16},{9,1},{17,9},{25,17},{10,2},{18,10},{26,18},{... | collective-permute-start | bytes 9224 | tf_op jit(solution)/shard_map/ppermute | solution.py:19
  105.2 17.8 %collective-permute-start.31 = (f32[3,8,1,128]{3,1,2,0:T(8,128)S(1)}, f32[3,8,1,128]{3,1,2,0:T(8,128)S(1)}, u32[]{:S(2)}, u32[]{:S(2)}) collective-permute-start(f32[3,8,1,128]{3,1,2,0:T(8,128)S(1)} %bitcast.84), channel_id=1, source_target_pairs={{0,4},{1,5},{2,6},{3,7},{8,12},{9,13},{10,14},{11,15},{16,20},{17,... | collective-permute-start | bytes 36872 | tf_op jit(solution)/shard_map/ppermute | solution.py:19
  109.7 13.2 %collective-permute-start.32 = (f32[3,1,32,128]{3,2,1,0:T(8,128)S(1)}, f32[3,1,32,128]{3,2,1,0:T(8,128)S(1)}, u32[]{:S(2)}, u32[]{:S(2)}) collective-permute-start(f32[3,1,32,128]{3,2,1,0:T(8,128)S(1)} %slice.700), channel_id=1, source_target_pairs={{0,1},{1,2},{2,3},{4,5},{5,6},{6,7},{8,9},{9,10},{10,11},{12,13},{... | collective-permute-start | bytes 147464 | tf_op jit(solution)/shard_map/ppermute | solution.py:19
  114.3 8.7 %collective-permute-start.30 = (f32[3,8,32,1]{3,2,1,0:T(8,128)S(1)}, f32[3,8,32,1]{3,2,1,0:T(8,128)S(1)}, u32[]{:S(2)}, u32[]{:S(2)}) collective-permute-start(f32[3,8,32,1]{3,2,1,0:T(8,128)S(1)} %slice.694), channel_id=1, source_target_pairs={{0,8},{8,16},{16,24},{1,9},{9,17},{17,25},{2,10},{10,18},{18,26},{... | collective-permute-start | bytes 9224 | tf_op jit(solution)/shard_map/ppermute | solution.py:19
  125.0 9.6 %collective-permute-start.35 = (f32[3,1,32,128]{3,2,1,0:T(8,128)S(1)}, f32[3,1,32,128]{3,2,1,0:T(8,128)S(1)}, u32[]{:S(2)}, u32[]{:S(2)}) collective-permute-start(f32[3,1,32,128]{3,2,1,0:T(8,128)S(1)} %fusion.133), channel_id=1, source_target_pairs={{1,0},{2,1},{3,2},{5,4},{6,5},{7,6},{9,8},{10,9},{11,10},{13,12},{... | collective-permute-start | bytes 147464 | tf_op jit(solution)/shard_map/ppermute | solution.py:19
  126.4 8.2 %collective-permute-start.34 = (f32[3,8,1,128]{3,1,2,0:T(8,128)S(1)}, f32[3,8,1,128]{3,1,2,0:T(8,128)S(1)}, u32[]{:S(2)}, u32[]{:S(2)}) collective-permute-start(f32[3,8,1,128]{3,1,2,0:T(8,128)S(1)} %bitcast.85), channel_id=1, source_target_pairs={{4,0},{5,1},{6,2},{7,3},{12,8},{13,9},{14,10},{15,11},{20,16},{21,... | collective-permute-start | bytes 36872 | tf_op jit(solution)/shard_map/ppermute | solution.py:19
  127.7 6.9 %collective-permute-start.33 = (f32[3,8,32,1]{3,2,1,0:T(8,128)S(1)}, f32[3,8,32,1]{3,2,1,0:T(8,128)S(1)}, u32[]{:S(2)}, u32[]{:S(2)}) collective-permute-start(f32[3,8,32,1]{3,2,1,0:T(8,128)S(1)} %fusion.4), channel_id=1, source_target_pairs={{8,0},{16,8},{24,16},{9,1},{17,9},{25,17},{10,2},{18,10},{26,18},{... | collective-permute-start | bytes 9224 | tf_op jit(solution)/shard_map/ppermute | solution.py:19
  135.9 18.3 %collective-permute-start.29 = (f32[1,1,32,128]{3,2,1,0:T(8,128)S(1)}, f32[1,1,32,128]{3,2,1,0:T(8,128)S(1)}, u32[]{:S(2)}, u32[]{:S(2)}) collective-permute-start(f32[1,1,32,128]{3,2,1,0:T(8,128)S(1)} %slice.692), channel_id=1, source_target_pairs={{0,1},{1,2},{2,3},{4,5},{5,6},{6,7},{8,9},{9,10},{10,11},{12,13},{... | collective-permute-start | bytes 49160 | tf_op jit(solution)/shard_map/ppermute | solution.py:19
  140.1 14.0 %collective-permute-start.28 = (f32[1,8,1,128]{3,2,1,0:T(1,128)S(1)}, f32[1,8,1,128]{3,2,1,0:T(1,128)S(1)}, u32[]{:S(2)}, u32[]{:S(2)}) collective-permute-start(f32[1,8,1,128]{3,2,1,0:T(1,128)S(1)} %slice.689), channel_id=1, source_target_pairs={{0,4},{1,5},{2,6},{3,7},{8,12},{9,13},{10,14},{11,15},{16,20},{17,... | collective-permute-start | bytes 12296 | tf_op jit(solution)/shard_map/ppermute | solution.py:19
  144.5 9.6 %collective-permute-start.27 = (f32[1,8,32,1]{3,2,1,0:T(8,128)S(1)}, f32[1,8,32,1]{3,2,1,0:T(8,128)S(1)}, u32[]{:S(2)}, u32[]{:S(2)}) collective-permute-start(f32[1,8,32,1]{3,2,1,0:T(8,128)S(1)} %slice.686), channel_id=1, source_target_pairs={{0,8},{8,16},{16,24},{1,9},{9,17},{17,25},{2,10},{10,18},{18,26},{... | collective-permute-start | bytes 3080 | tf_op jit(solution)/shard_map/ppermute | solution.py:19
  (13 other events, 63.2 us)
where the time goes:
time: 157 us; the launch traced here: 155 us
  starting transfers between devices  109 us (69%)
  waiting for transfers between devices  28.9 us (18%)
  other arithmetic  7.78 us (5%)
  local copies, waits for them, and re-layouts  7.72 us (5%)
  between operations  1.93 us (1%)
    ppermute x36, starting transfers between devices, passed_along(): return lax.ppermute(shard, axis, pairs)  109 us
    ppermute x36, waiting for transfers between devices, passed_along(): return lax.ppermute(shard, axis, pairs)  28.9 us
  transfers between devices with their start and end apart: 36, of which 12 were waited for; matrix products, arithmetic and copies ran while one was open for 3% of the time, Pallas kernels for 0%

commit v1 on v0

v1 whole, which is shorter than its diff:
```python
import functools

import jax
import jax.numpy as jnp
from jax import lax
from jax.experimental import pallas as pl
from jax.experimental.pallas import tpu as pltpu
from jax.sharding import PartitionSpec as P

ITERS = 3
AXES = ("gx", "gy", "gz")
ALPHA1, ALPHA0, SIGMA, TAU = 0.5, 1.0, 0.2, 0.2
Q_FROM = (0, 3, 1, 5, 2, 4)
XX, XY, YY, YZ, ZZ, XZ = range(6)
MESH = pl.DeviceIdType.MESH
TOP = 8


def kernel(
    noisy_in, fid_in, u_in, v_in, p_in, q_in,
    u_out, v_out, p_out, q_out,
    bar, pp, qq, gain, offset,
    send_u, send_v, send_p, send_q, got_u, got_v, got_p, got_q,
    load_sem, send_sem, recv_sem,
):
    zs, ys, xs = u_in.shape
    blocks = ys // 8
    place = [lax.axis_index(a) for a in AXES]
    count = [lax.axis_size(a) for a in AXES]
    below = [place[i] > 0 for i in range(3)]
    above = [place[i] < count[i] - 1 for i in range(3)]

    peers = sum(there.astype(jnp.int32) for there in below + above)

    barrier = pltpu.get_barrier_semaphore()
    for i in range(3):
        for there, by in ((below[i], -1), (above[i], 1)):
            @pl.when(there)
            def _():
                pl.semaphore_signal(
                    barrier, inc=1, device_id={AXES[i]: place[i] + by}, device_id_type=MESH
                )

    mid_z, mid_y = pl.ds(1, zs), pl.ds(TOP, ys)
    loads = [
        pltpu.make_async_copy(u_in, bar.at[0, mid_z, mid_y], load_sem.at[0]),
        pltpu.make_async_copy(v_in, bar.at[pl.ds(1, 3), mid_z, mid_y], load_sem.at[1]),
        pltpu.make_async_copy(p_in, pp.at[:, mid_z, mid_y], load_sem.at[2]),
        pltpu.make_async_copy(noisy_in, offset, load_sem.at[3]),
        pltpu.make_async_copy(fid_in, gain, load_sem.at[4]),
    ] + [
        pltpu.make_async_copy(q_in.at[Q_FROM[k]], qq.at[k, mid_z, mid_y], load_sem.at[5 + k])
        for k in range(6)
    ]
    for load in loads:
        load.start()

    row = jnp.zeros((zs + 2, 1, xs), jnp.float32)
    layer = jnp.zeros((ys, xs), jnp.float32)

    @pl.when(jnp.logical_not(below[0]))
    def _():
        got_v[...] = layer
        got_p[...] = layer

    @pl.when(jnp.logical_not(above[0]))
    def _():
        got_u[...] = layer
        got_q[...] = layer

    @pl.when(jnp.logical_not(below[1]))
    def _():
        for k in range(3):
            bar[1 + k, :, TOP - 1 : TOP, :] = row
        pp[1, :, TOP - 1 : TOP, :] = row

    @pl.when(jnp.logical_not(above[1]))
    def _():
        bar[0, :, TOP + ys : TOP + ys + 1, :] = row
        for k in (XY, YY, YZ):
            qq[k, :, TOP + ys : TOP + ys + 1, :] = row

    @pl.when(jnp.logical_not(below[2]))
    def _():
        for k in range(3):
            bar[1 + k, 0, TOP : TOP + ys, :] = layer
        pp[2, 0, TOP : TOP + ys, :] = layer

    @pl.when(jnp.logical_not(above[2]))
    def _():
        bar[0, zs + 1, TOP : TOP + ys, :] = layer
        for k in (YZ, ZZ, XZ):
            qq[k, zs + 1, TOP : TOP + ys, :] = layer

    lane = lax.broadcasted_iota(jnp.int32, (8, xs), 1)
    sub = lax.broadcasted_iota(jnp.int32, (8, xs), 0)
    first_lane, last_lane = lane == 0, lane == xs - 1

    def factor(flag):
        return jnp.where(flag, jnp.float32(1), jnp.float32(0))

    up_x = jnp.where(last_lane, factor(above[0]), 1.0)
    lo_x = jnp.where(first_lane, factor(below[0]), 1.0)
    up_y_last = jnp.where(sub == 7, factor(above[1]), 1.0)
    lo_y_first = jnp.where(sub == 0, factor(below[1]), 1.0)

    def up_z(z):
        return jnp.where(jnp.logical_or(z < zs - 1, above[2]), jnp.float32(1), jnp.float32(0))

    def lo_z(z):
        return jnp.where(jnp.logical_or(z > 0, below[2]), jnp.float32(1), jnp.float32(0))

    def up_y(b, value):
        return up_y_last * value if b == blocks - 1 else value

    def lo_y(b, value):
        return lo_y_first * value if b == 0 else value

    def next_x(value, got, k, z):
        return jnp.where(
            last_lane, pltpu.roll(got, xs - 1 - k * zs - z, 1), pltpu.roll(value, xs - 1, 1)
        )

    def prev_x(value, got, k, z):
        return jnp.where(
            first_lane, pltpu.roll(got, xs - 1 - k * zs - z, 1), pltpu.roll(value, 1, 1)
        )

    def pack_first(packed, value, k, z):
        return jnp.where(lane == k * zs + z, pltpu.roll(value, k * zs + z, 1), packed)

    def pack_last(packed, value, k, z):
        return jnp.where(lane == k * zs + z + 1, pltpu.roll(value, k * zs + z + 2, 1), packed)

    def down(src, dst, i, k):
        return (
            pltpu.make_async_remote_copy(
                src_ref=src, dst_ref=dst, send_sem=send_sem.at[k], recv_sem=recv_sem.at[k],
                device_id={AXES[i]: place[i] - 1}, device_id_type=MESH,
            ),
            below[i],
            above[i],
        )

    def up(src, dst, i, k):
        return (
            pltpu.make_async_remote_copy(
                src_ref=src, dst_ref=dst, send_sem=send_sem.at[k], recv_sem=recv_sem.at[k],
                device_id={AXES[i]: place[i] + 1}, device_id_type=MESH,
            ),
            above[i],
            below[i],
        )

    comps = pl.ds(1, 3)
    primal_moves = [
        up(bar.at[comps, zs, mid_y], bar.at[comps, 0, mid_y], 2, 0),
        down(bar.at[0, 1, mid_y], bar.at[0, zs + 1, mid_y], 2, 1),
        up(bar.at[comps, mid_z, TOP + ys - 1], bar.at[comps, mid_z, TOP - 1], 1, 2),
        down(bar.at[0, mid_z, TOP], bar.at[0, mid_z, TOP + ys], 1, 3),
        up(send_v, got_v, 0, 4),
        down(send_u, got_u, 0, 5),
    ]
    dual_moves = [
        down(qq.at[pl.ds(YZ, 3), 1, mid_y], qq.at[pl.ds(YZ, 3), zs + 1, mid_y], 2, 6),
        up(pp.at[2, zs, mid_y], pp.at[2, 0, mid_y], 2, 7),
        down(qq.at[pl.ds(XY, 3), mid_z, TOP], qq.at[pl.ds(XY, 3), mid_z, TOP + ys], 1, 8),
        up(pp.at[1, mid_z, TOP + ys - 1], pp.at[1, mid_z, TOP - 1], 1, 9),
        down(send_q, got_q, 0, 10),
        up(send_p, got_p, 0, 11),
    ]

    def start(moves):
        for copy, goes, comes in moves:
            @pl.when(goes)
            def _():
                copy.start()

    def finish(moves):
        for copy, goes, comes in moves:
            @pl.when(goes)
            def _():
                copy.wait_send()

            @pl.when(comes)
            def _():
                copy.wait_recv()

    empty = jnp.zeros((8, xs), jnp.float32)

    def rows(b, by=0):
        return pl.ds(TOP + 8 * b + by, 8)

    def store_packed(ref, packed):
        for b in range(blocks):
            ref[pl.ds(8 * b, 8), :] = packed[b]

    for load in loads[:2]:
        load.wait()

    def first_faces(z, packed):
        first, last = list(packed[0]), list(packed[1])
        for b in range(blocks):
            first[b] = pack_first(first[b], bar[0, z + 1, rows(b), :], 0, z)
            for k in range(3):
                last[b] = pack_last(last[b], bar[1 + k, z + 1, rows(b), :], k, z)
        return tuple(first), tuple(last)

    nothing = (empty,) * blocks
    first, last = lax.fori_loop(0, zs, first_faces, (nothing, nothing))
    store_packed(send_u, first)
    store_packed(send_v, last)
    pl.semaphore_wait(barrier, peers)
    start(primal_moves)

    for load in loads[2:]:
        load.wait()

    def prepare(z, carry):
        weight = TAU * gain[z]
        inverse = 1.0 / (1.0 + weight)
        gain[z] = inverse
        offset[z] = weight * offset[z] * inverse
        return carry

    lax.fori_loop(0, zs, prepare, 0)

    for step in range(ITERS):
        last_step = step == ITERS - 1
        finish(primal_moves)

        def dual(z, packed):
            of_p, of_q = list(packed[0]), list(packed[1])
            z_up, z_lo = SIGMA * up_z(z), (0.5 * SIGMA) * lo_z(z)
            for b in range(blocks):
                r, here = rows(b), pl.ds(8 * b, 8)
                u = bar[0, z + 1, r, :]
                v = [bar[1 + k, z + 1, r, :] for k in range(3)]
                t = [
                    pp[0, z + 1, r, :] + SIGMA * (up_x * (next_x(u, got_u[here, :], 0, z) - u) - v[0]),
                    pp[1, z + 1, r, :]
                    + SIGMA * (up_y(b, bar[0, z + 1, rows(b, 1), :] - u) - v[1]),
                    pp[2, z + 1, r, :] + (z_up * (bar[0, z + 2, r, :] - u) - SIGMA * v[2]),
                ]
                size = t[0] * t[0] + t[1] * t[1] + t[2] * t[2]
                scale = jnp.minimum(1.0, ALPHA1 * lax.rsqrt(size))
                t = [scale * part for part in t]
                for k in range(3):
                    pp[k, z + 1, r, :] = t[k]
                    if last_step:
                        p_out[k, z, here, :] = t[k]
                of_p[b] = pack_last(of_p[b], t[0], 0, z)

                half_lo_x = (0.5 * SIGMA) * lo_x
                received = got_v[here, :]
                dx = [half_lo_x * (v[k] - prev_x(v[k], received, k, z)) for k in range(3)]
                dy = [
                    lo_y(b, (0.5 * SIGMA) * (v[k] - bar[1 + k, z + 1, rows(b, -1), :]))
                    for k in range(3)
                ]
                dz = [z_lo * (v[k] - bar[1 + k, z, r, :]) for k in range(3)]
                s = [None] * 6
                s[XX] = qq[XX, z + 1, r, :] + 2.0 * dx[0]
                s[YY] = qq[YY, z + 1, r, :] + 2.0 * dy[1]
                s[ZZ] = qq[ZZ, z + 1, r, :] + 2.0 * dz[2]
                s[XY] = qq[XY, z + 1, r, :] + (dy[0] + dx[1])
                s[XZ] = qq[XZ, z + 1, r, :] + (dz[0] + dx[2])
                s[YZ] = qq[YZ, z + 1, r, :] + (dz[1] + dy[2])
                size = (s[XX] * s[XX] + s[YY] * s[YY] + s[ZZ] * s[ZZ]) + 2.0 * (
                    s[XY] * s[XY] + s[XZ] * s[XZ] + s[YZ] * s[YZ]
                )
                scale = jnp.minimum(1.0, ALPHA0 * lax.rsqrt(size))
                s = [scale * part for part in s]
                for k in range(6):
                    qq[k, z + 1, r, :] = s[k]
                    if last_step:
                        q_out[Q_FROM[k], z, here, :] = s[k]
                for k, part in enumerate((XX, XY, XZ)):
                    of_q[b] = pack_first(of_q[b], s[part], k, z)
            return tuple(of_p), tuple(of_q)

        of_p, of_q = lax.fori_loop(0, zs, dual, (nothing, nothing))
        store_packed(send_p, of_p)
        store_packed(send_q, of_q)
        start(dual_moves)
        finish(dual_moves)

        def primal(z, packed):
            of_u, of_v = list(packed[0]), list(packed[1])
            z_up, z_lo = up_z(z), lo_z(z)
            for b in range(blocks):
                r, here = rows(b), pl.ds(8 * b, 8)
                p = [pp[k, z + 1, r, :] for k in range(3)]
                div = (
                    (up_x * p[0] - prev_x(p[0], got_p[here, :], 0, z))
                    + (up_y(b, p[1]) - pp[1, z + 1, rows(b, -1), :])
                    + (z_up * p[2] - pp[2, z, r, :])
                )
                q = [qq[k, z + 1, r, :] for k in range(6)]
                received = got_q[here, :]
                new_v = []
                for k, (ax, ay, az) in enumerate(((XX, XY, XZ), (XY, YY, YZ), (XZ, YZ, ZZ))):
                    div2 = (
                        (next_x(q[ax], received, k, z) - lo_x * q[ax])
                        + (qq[ay, z + 1, rows(b, 1), :] - lo_y(b, q[ay]))
                        + (qq[az, z + 2, r, :] - z_lo * q[az])
                    )
                    old = bar[1 + k, z + 1, r, :] if step == 0 else v_out[k, z, here, :]
                    new = old + TAU * (p[k] + div2)
                    v_out[k, z, here, :] = new
                    if not last_step:
                        ahead = 2.0 * new - old
                        bar[1 + k, z + 1, r, :] = ahead
                        of_v[b] = pack_last(of_v[b], ahead, k, z)
                old = bar[0, z + 1, r, :] if step == 0 else u_out[z, here, :]
                new = (old + TAU * div) * gain[z, here, :] + offset[z, here, :]
                u_out[z, here, :] = new
                if not last_step:
                    ahead = 2.0 * new - old
                    bar[0, z + 1, r, :] = ahead
                    of_u[b] = pack_first(of_u[b], ahead, 0, z)
            return tuple(of_u), tuple(of_v)

        of_u, of_v = lax.fori_loop(0, zs, primal, (nothing, nothing))
        if not last_step:
            store_packed(send_u, of_u)
            store_packed(send_v, of_v)
            start(primal_moves)


def per_device(noisy_image, fidelity, primal_u, primal_v, dual_p, dual_q):
    zs, ys, xs = primal_u.shape
    assert xs == 128 and ys % 8 == 0 and 3 * zs < xs
    f32 = jnp.float32
    padded = (zs + 2, ys + 2 * TOP, xs)
    face = pltpu.VMEM((ys, xs), f32)
    return pl.pallas_call(
        kernel,
        out_shape=tuple(pltpu.VMEM(a.shape, f32) for a in (primal_u, primal_v, dual_p, dual_q)),
        in_specs=[pl.BlockSpec(memory_space=pl.ANY)] * 6,
        out_specs=tuple([pl.BlockSpec(memory_space=pltpu.VMEM)] * 4),
        scratch_shapes=[
            pltpu.VMEM((4,) + padded, f32),
            pltpu.VMEM((3,) + padded, f32),
            pltpu.VMEM((6,) + padded, f32),
            pltpu.VMEM((zs, ys, xs), f32),
            pltpu.VMEM((zs, ys, xs), f32),
        ]
        + [face] * 8
        + [
            pltpu.SemaphoreType.DMA((11,)),
            pltpu.SemaphoreType.DMA((12,)),
            pltpu.SemaphoreType.DMA((12,)),
        ],
        compiler_params=pltpu.CompilerParams(collective_id=0, has_side_effects=True),
        name="tgv",
    )(noisy_image, fidelity, primal_u, primal_v, dual_p, dual_q)


def solution(mesh):
    scalar, stack = P("gz", "gy", "gx"), P(None, "gz", "gy", "gx")
    return jax.shard_map(
        per_device,
        mesh=mesh,
        in_specs=(scalar, scalar, scalar, stack, stack, stack),
        out_specs=(scalar, stack, stack, stack),
        check_vma=False,
    )
```

time: 157 us -> 35.9 us (0.23); the launches traced: 155 us -> 35.7 us
  starting transfers between devices: 109 us -> 0 us
  Pallas kernels: 0 us -> 32 us
  waiting for transfers between devices: 28.9 us -> 0 us
  other arithmetic: 7.78 us -> 0 us
  local copies, waits for them, and re-layouts: 7.72 us -> 3.03 us
    ppermute x36 -> x0, starting transfers between devices: 109 us -> none  [passed_along(): return lax.ppermute(shard, axis, pairs)]
    pallas_call x0 -> x1, Pallas kernels: none -> 32 us  [per_device(): pl.pallas_call(kernel, out_shape=tuple((pltpu.VMEM(a.shape, f32) for a in...]
    ppermute x36 -> x0, waiting for transfers between devices: 28.9 us -> none  [passed_along(): return lax.ppermute(shard, axis, pairs)]
    slice x54 -> x0, local copies, waits for them, and re-layouts: 4.94 us -> none  [the longest x18 2.54 us: last_layer(): return lax.slice_in_dim(values, extent - 1, extent, axis=axis_dim)]
    reduce_sum x5 -> x0, other arithmetic: 1.77 us -> none  [project(): jnp.sum(weights * stacked * stacked, axis=0, keepdims=True)]
  transfers between devices with their start and end apart: 36 -> 0, of which waited for: 12 -> 0; matrix products, arithmetic and copies ran while one was open for 3% -> 0% of each run, Pallas kernels for 0% -> 0%
where the time goes in v1:
time: 35.9 us; the launch traced here: 35.7 us
  Pallas kernels  32 us (89%)
  local copies, waits for them, and re-layouts  3.03 us (8%)
  between operations  0.64 us (2%)
    pallas_call x1, Pallas kernels, per_device(): pl.pallas_call(kernel, out_shape=tuple((pltpu.VMEM(a.shape, f32) for a in...  32 us
    unnamed x4, local copies, waits for them, and re-layouts  3.03 us

profile of v1, /device:TPU:0, one launch (start us, length us, event | category | flops | bytes accessed | tf_op | source)
XLA Modules:
  0.0 35.7 jit_solution(8609189415023009946)
XLA Ops:
  0.6 32.0 %tgv.1 = (f32[8,32,128]{2,1,0:T(8,128)S(1)}, f32[3,8,32,128]{3,2,1,0:T(8,128)S(1)}, f32[3,8,32,128]{3,2,1,0:T(8,128)S(1)}, f32[6,8,32,128]{3,2,1,0:T(8,128)S(1)}) custom-call(f32[8,32,128]{2,1,0:T(8,128)} %noisy_in.1, f32[8,32,128]{2,1,0:T(8,128)} %fid_in.1, f32[8,32,128]{2,1,0:T(8,128)} %u_in.1, f32[3,8,32,128]{3,2,1,0:T(8,128)} %v_in.1, ...), custom_call_target="tpu_custom_call" | custom-call | tf_op jit(solution)/shard_map/tgv/pallas_call | solution.py:337
  32.7 0.7 %copy.14 = f32[8,32,128]{2,1,0:T(8,128)} copy(f32[8,32,128]{2,1,0:T(8,128)S(1)} %get-tuple-element.4) | data formatting | bytes 262144
  33.3 0.7 %copy.15 = f32[3,8,32,128]{3,2,1,0:T(8,128)} copy(f32[3,8,32,128]{3,2,1,0:T(8,128)S(1)} %get-tuple-element.5) | data formatting | bytes 786432
  34.1 0.7 %copy.16 = f32[3,8,32,128]{3,2,1,0:T(8,128)} copy(f32[3,8,32,128]{3,2,1,0:T(8,128)S(1)} %get-tuple-element.6) | data formatting | bytes 786432
  34.8 0.9 %copy.17 = f32[6,8,32,128]{3,2,1,0:T(8,128)} copy(f32[6,8,32,128]{3,2,1,0:T(8,128)S(1)} %get-tuple-element.7) | data formatting | bytes 1572864

commit v2 on v1

--- a/solution.py
+++ b/solution.py
@@ -11,6 +11,7 @@
 AXES = ("gx", "gy", "gz")
 ALPHA1, ALPHA0, SIGMA, TAU = 0.5, 1.0, 0.2, 0.2
 Q_FROM = (0, 3, 1, 5, 2, 4)
+GROUP = 4
 XX, XY, YY, YZ, ZZ, XZ = range(6)
 MESH = pl.DeviceIdType.MESH
 TOP = 8
@@ -104,11 +105,30 @@
     up_y_last = jnp.where(sub == 7, factor(above[1]), 1.0)
     lo_y_first = jnp.where(sub == 0, factor(below[1]), 1.0)
 
+    def flush(later):
+        for ref, at, value in later:
+            ref[at + (slice(None),)] = value
+        later.clear()
+
+    def sweep(body, moves, wanted):
+        def turn(j, packed):
+            one, two = list(packed[0]), list(packed[1])
+            body(jnp.where(j == 0, 0, 2 * j - 1), one, two)
+            body(jnp.where(j == 0, zs - 1, 2 * j), one, two)
+
+            @pl.when(jnp.logical_and(wanted, j == 0))
+            def _():
+                start(moves)
+
+            return tuple(one), tuple(two)
+
+        return lax.fori_loop(0, zs // 2, turn, (nothing, nothing))
+
     def up_z(z):
-        return jnp.where(jnp.logical_or(z < zs - 1, above[2]), jnp.float32(1), jnp.float32(0))
+        return factor(jnp.logical_or(z < zs - 1, above[2]))
 
     def lo_z(z):
-        return jnp.where(jnp.logical_or(z > 0, below[2]), jnp.float32(1), jnp.float32(0))
+        return factor(jnp.logical_or(z > 0, below[2]))
 
     def up_y(b, value):
         return up_y_last * value if b == blocks - 1 else value
@@ -221,18 +241,23 @@
         inverse = 1.0 / (1.0 + weight)
         gain[z] = inverse
         offset[z] = weight * offset[z] * inverse
+        u_out[z] = bar[0, z + 1, mid_y, :]
+        for k in range(3):
+            v_out[k, z] = bar[1 + k, z + 1, mid_y, :]
         return carry
 
     lax.fori_loop(0, zs, prepare, 0)
 
-    for step in range(ITERS):
-        last_step = step == ITERS - 1
+    def iteration(step, carry):
+        more = step < ITERS - 1
         finish(primal_moves)
 
-        def dual(z, packed):
-            of_p, of_q = list(packed[0]), list(packed[1])
+        def dual(z, of_p, of_q):
             z_up, z_lo = SIGMA * up_z(z), (0.5 * SIGMA) * lo_z(z)
+            later = []
             for b in range(blocks):
+                if b % GROUP == 0:
+                    flush(later)
                 r, here = rows(b), pl.ds(8 * b, 8)
                 u = bar[0, z + 1, r, :]
                 v = [bar[1 + k, z + 1, r, :] for k in range(3)]
@@ -246,9 +271,8 @@
                 scale = jnp.minimum(1.0, ALPHA1 * lax.rsqrt(size))
                 t = [scale * part for part in t]
                 for k in range(3):
-                    pp[k, z + 1, r, :] = t[k]
-                    if last_step:
-                        p_out[k, z, here, :] = t[k]
+                    later.append((pp, (k, z + 1, r), t[k]))
+                    later.append((p_out, (k, z, here), t[k]))
                 of_p[b] = pack_last(of_p[b], t[0], 0, z)
 
                 half_lo_x = (0.5 * SIGMA) * lo_x
@@ -272,23 +296,24 @@
                 scale = jnp.minimum(1.0, ALPHA0 * lax.rsqrt(size))
                 s = [scale * part for part in s]
                 for k in range(6):
-                    qq[k, z + 1, r, :] = s[k]
-                    if last_step:
-                        q_out[Q_FROM[k], z, here, :] = s[k]
+                    later.append((qq, (k, z + 1, r), s[k]))
+                    later.append((q_out, (Q_FROM[k], z, here), s[k]))
                 for k, part in enumerate((XX, XY, XZ)):
                     of_q[b] = pack_first(of_q[b], s[part], k, z)
-            return tuple(of_p), tuple(of_q)
-
-        of_p, of_q = lax.fori_loop(0, zs, dual, (nothing, nothing))
+            flush(later)
+
+        of_p, of_q = sweep(dual, dual_moves[:2], True)
         store_packed(send_p, of_p)
         store_packed(send_q, of_q)
-        start(dual_moves)
+        start(dual_moves[2:])
         finish(dual_moves)
 
-        def primal(z, packed):
-            of_u, of_v = list(packed[0]), list(packed[1])
+        def primal(z, of_u, of_v):
             z_up, z_lo = up_z(z), lo_z(z)
+            later = []
             for b in range(blocks):
+                if b % GROUP == 0:
+                    flush(later)
                 r, here = rows(b), pl.ds(8 * b, 8)
                 p = [pp[k, z + 1, r, :] for k in range(3)]
                 div = (
@@ -305,36 +330,49 @@
                         + (qq[ay, z + 1, rows(b, 1), :] - lo_y(b, q[ay]))
                         + (qq[az, z + 2, r, :] - z_lo * q[az])
                     )
-                    old = bar[1 + k, z + 1, r, :] if step == 0 else v_out[k, z, here, :]
+                    old = v_out[k, z, here, :]
                     new = old + TAU * (p[k] + div2)
-                    v_out[k, z, here, :] = new
-                    if not last_step:
-                        ahead = 2.0 * new - old
-                        bar[1 + k, z + 1, r, :] = ahead
-                        of_v[b] = pack_last(of_v[b], ahead, k, z)
-                old = bar[0, z + 1, r, :] if step == 0 else u_out[z, here, :]
+                    later.append((v_out, (k, z, here), new))
+                    ahead = 2.0 * new - old
+                    later.append((bar, (1 + k, z + 1, r), ahead))
+                    of_v[b] = pack_last(of_v[b], ahead, k, z)
+                old = u_out[z, here, :]
                 new = (old + TAU * div) * gain[z, here, :] + offset[z, here, :]
-                u_out[z, here, :] = new
-                if not last_step:
-                    ahead = 2.0 * new - old
-                    bar[0, z + 1, r, :] = ahead
-                    of_u[b] = pack_first(of_u[b], ahead, 0, z)
-            return tuple(of_u), tuple(of_v)
-
-        of_u, of_v = lax.fori_loop(0, zs, primal, (nothing, nothing))
-        if not last_step:
+                later.append((u_out, (z, here), new))
+                ahead = 2.0 * new - old
+                later.append((bar, (0, z + 1, r), ahead))
+                of_u[b] = pack_first(of_u[b], ahead, 0, z)
+            flush(later)
+
+        of_u, of_v = sweep(primal, primal_moves[:2], more)
+
+        @pl.when(more)
+        def _():
             store_packed(send_u, of_u)
             store_packed(send_v, of_v)
-            start(primal_moves)
+            start(primal_moves[2:])
+
+        return carry
+
+    lax.fori_loop(0, ITERS, iteration, 0)
+
+
+def copy_out(u_in, v_in, p_in, q_in, u_out, v_out, p_out, q_out, sems):
+    pairs = ((q_in, q_out), (p_in, p_out), (v_in, v_out), (u_in, u_out))
+    copies = [pltpu.make_async_copy(a, b, sems.at[i]) for i, (a, b) in enumerate(pairs)]
+    for copy in copies:
+        copy.start()
+    for copy in copies:
+        copy.wait()
 
 
 def per_device(noisy_image, fidelity, primal_u, primal_v, dual_p, dual_q):
     zs, ys, xs = primal_u.shape
-    assert xs == 128 and ys % 8 == 0 and 3 * zs < xs
+    assert xs == 128 and ys % 8 == 0 and zs % 2 == 0 and 3 * zs < xs
     f32 = jnp.float32
     padded = (zs + 2, ys + 2 * TOP, xs)
     face = pltpu.VMEM((ys, xs), f32)
-    return pl.pallas_call(
+    results = pl.pallas_call(
         kernel,
         out_shape=tuple(pltpu.VMEM(a.shape, f32) for a in (primal_u, primal_v, dual_p, dual_q)),
         in_specs=[pl.BlockSpec(memory_space=pl.ANY)] * 6,
@@ -355,6 +393,14 @@
         compiler_params=pltpu.CompilerParams(collective_id=0, has_side_effects=True),
         name="tgv",
     )(noisy_image, fidelity, primal_u, primal_v, dual_p, dual_q)
+    return pl.pallas_call(
+        copy_out,
+        out_shape=tuple(jax.ShapeDtypeStruct(a.shape, f32) for a in results),
+        in_specs=[pl.BlockSpec(memory_space=pltpu.VMEM)] * 4,
+        out_specs=tuple([pl.BlockSpec(memory_space=pl.ANY)] * 4),
+        scratch_shapes=[pltpu.SemaphoreType.DMA((4,))],
+        name="out",
+    )(*[pltpu.with_memory_space_constraint(r, pltpu.VMEM) for r in results])
 
 
 def solution(mesh):

time: 35.9 us -> 28.9 us (0.81)
  Pallas kernels: 32 us -> 28.1 us
  local copies, waits for them, and re-layouts: 3.03 us -> 0 us
    pallas_call x1, Pallas kernels: 32 us -> 26.9 us  [per_device(): pl.pallas_call(kernel, out_shape=tuple((pltpu.VMEM(a.shape, f32) for a in...]
    unnamed x4 -> x0, local copies, waits for them, and re-layouts: 3.03 us -> none
    pallas_call x0 -> x1, Pallas kernels: none -> 1.21 us  [per_device(): pl.pallas_call(copy_out, out_shape=tuple((jax.ShapeDtypeStruct(a.shape, f...]
where the time goes in v2:
time: 28.9 us; the launch traced here: 28.8 us
  Pallas kernels  28.1 us (97%)
  between operations  0.64 us (2%)
    pallas_call x1, Pallas kernels, per_device(): pl.pallas_call(kernel, out_shape=tuple((pltpu.VMEM(a.shape, f32) for a in...  26.9 us
    pallas_call x1, Pallas kernels, per_device(): pl.pallas_call(copy_out, out_shape=tuple((jax.ShapeDtypeStruct(a.shape, f...  1.21 us

profile of v2, /device:TPU:0, one launch (start us, length us, event | category | flops | bytes accessed | tf_op | source)
XLA Modules:
  0.0 28.8 jit_solution(14115902270839059368)
XLA Ops:
  0.6 26.9 %tgv.1 = (f32[8,32,128]{2,1,0:T(8,128)S(1)}, f32[3,8,32,128]{3,2,1,0:T(8,128)S(1)}, f32[3,8,32,128]{3,2,1,0:T(8,128)S(1)}, f32[6,8,32,128]{3,2,1,0:T(8,128)S(1)}) custom-call(f32[8,32,128]{2,1,0:T(8,128)} %noisy_in.1, f32[8,32,128]{2,1,0:T(8,128)} %fid_in.1, f32[8,32,128]{2,1,0:T(8,128)} %u_in.1, f32[3,8,32,128]{3,2,1,0:T(8,128)} %v_in.1, ...), custom_call_target="tpu_custom_call" | custom-call | tf_op jit(solution)/shard_map/tgv/pallas_call | solution.py:375
  27.6 1.2 %out.1 = (f32[8,32,128]{2,1,0:T(8,128)}, f32[3,8,32,128]{3,2,1,0:T(8,128)}, f32[3,8,32,128]{3,2,1,0:T(8,128)}, f32[6,8,32,128]{3,2,1,0:T(8,128)}) custom-call(f32[8,32,128]{2,1,0:T(8,128)S(1)} %get-tuple-element.8.u_in, f32[3,8,32,128]{3,2,1,0:T(8,128)S(1)} %get-tuple-element.9.v_in, f32[3,8,32,128]{3,2,1,0:T(8,128)S(1)} %get-tuple-element.10.p_in, ...), custom_call_target="tpu_custom_call" | custom-call | tf_op jit(solution)/shard_map/out/pallas_call | solution.py:396

commit v3 on v2

--- a/solution.py
+++ b/solution.py
@@ -20,7 +20,7 @@
 def kernel(
     noisy_in, fid_in, u_in, v_in, p_in, q_in,
     u_out, v_out, p_out, q_out,
-    bar, pp, qq, gain, offset,
+    bar, pp, qq, gain, offset, partial,
     send_u, send_v, send_p, send_q, got_u, got_v, got_p, got_q,
     load_sem, send_sem, recv_sem,
 ):
@@ -110,6 +110,14 @@
             ref[at + (slice(None),)] = value
         later.clear()
 
+    def each(body):
+        def turn(j, carry):
+            body(2 * j)
+            body(2 * j + 1)
+            return carry
+
+        lax.fori_loop(0, zs // 2, turn, 0)
+
     def sweep(body, moves, wanted):
         def turn(j, packed):
             one, two = list(packed[0]), list(packed[1])
@@ -136,15 +144,39 @@
     def lo_y(b, value):
         return lo_y_first * value if b == 0 else value
 
-    def next_x(value, got, k, z):
-        return jnp.where(
-            last_lane, pltpu.roll(got, xs - 1 - k * zs - z, 1), pltpu.roll(value, xs - 1, 1)
-        )
-
-    def prev_x(value, got, k, z):
-        return jnp.where(
-            first_lane, pltpu.roll(got, xs - 1 - k * zs - z, 1), pltpu.roll(value, 1, 1)
-        )
+    def next_x(value):
+        return jnp.where(last_lane, 0.0, pltpu.roll(value, xs - 1, 1))
+
+    def prev_x(value):
+        return jnp.where(first_lane, 0.0, pltpu.roll(value, 1, 1))
+
+    def halo_next_x(got, k, z):
+        return jnp.where(last_lane, pltpu.roll(got, xs - 1 - k * zs - z, 1), 0.0)
+
+    def halo_prev_x(got, k, z):
+        return jnp.where(first_lane, pltpu.roll(got, xs - 1 - k * zs - z, 1), 0.0)
+
+    def next_y(ref, k, z, b, value):
+        if b < blocks - 1:
+            return ref[k, z + 1, rows(b, 1), :]
+        return jnp.where(sub == 7, 0.0, pltpu.roll(value, 7, 0))
+
+    def prev_y(ref, k, z, b, value):
+        if b > 0:
+            return ref[k, z + 1, rows(b, -1), :]
+        return jnp.where(sub == 0, 0.0, pltpu.roll(value, 1, 0))
+
+    def halo_next_y(ref, k, z, b):
+        return jnp.where(sub == 7, ref[k, z + 1, rows(b, 1), :], 0.0)
+
+    def halo_prev_y(ref, k, z, b):
+        return jnp.where(sub == 0, ref[k, z + 1, rows(b, -1), :], 0.0)
+
+    def next_z(ref, k, z, b):
+        return factor(z < zs - 1) * ref[k, jnp.minimum(z + 2, zs), rows(b), :]
+
+    def prev_z(ref, k, z, b):
+        return factor(z > 0) * ref[k, jnp.maximum(z, 1), rows(b), :]
 
     def pack_first(packed, value, k, z):
         return jnp.where(lane == k * zs + z, pltpu.roll(value, k * zs + z, 1), packed)
@@ -250,23 +282,46 @@
 
     def iteration(step, carry):
         more = step < ITERS - 1
+
+        def dual_inside(z):
+            later = []
+            z_up, z_lo = up_z(z), lo_z(z)
+            for b in range(blocks):
+                r = rows(b)
+                u = bar[0, z + 1, r, :]
+                v = [bar[1 + k, z + 1, r, :] for k in range(3)]
+                slopes = (
+                    next_x(u) - up_x * u,
+                    next_y(bar, 0, z, b, u) - up_y(b, u),
+                    next_z(bar, 0, z, b) - z_up * u,
+                )
+                for k in range(3):
+                    later.append((pp, (k, z + 1, r), pp[k, z + 1, r, :] + SIGMA * (slopes[k] - v[k])))
+                dx = [lo_x * v[k] - prev_x(v[k]) for k in range(3)]
+                dy = [lo_y(b, v[k]) - prev_y(bar, 1 + k, z, b, v[k]) for k in range(3)]
+                dz = [z_lo * v[k] - prev_z(bar, 1 + k, z, b) for k in range(3)]
+                half = 0.5 * SIGMA
+                for k, add in (
+                    (XX, SIGMA * dx[0]), (YY, SIGMA * dy[1]), (ZZ, SIGMA * dz[2]),
+                    (XY, half * (dy[0] + dx[1])), (XZ, half * (dz[0] + dx[2])),
+                    (YZ, half * (dz[1] + dy[2])),
+                ):
+                    later.append((qq, (k, z + 1, r), qq[k, z + 1, r, :] + add))
+            flush(later)
+
+        each(dual_inside)
         finish(primal_moves)
 
         def dual(z, of_p, of_q):
-            z_up, z_lo = SIGMA * up_z(z), (0.5 * SIGMA) * lo_z(z)
+            z_end, z_begin, half = SIGMA * factor(z == zs - 1), factor(z == 0), 0.5 * SIGMA
             later = []
             for b in range(blocks):
-                if b % GROUP == 0:
-                    flush(later)
                 r, here = rows(b), pl.ds(8 * b, 8)
-                u = bar[0, z + 1, r, :]
-                v = [bar[1 + k, z + 1, r, :] for k in range(3)]
-                t = [
-                    pp[0, z + 1, r, :] + SIGMA * (up_x * (next_x(u, got_u[here, :], 0, z) - u) - v[0]),
-                    pp[1, z + 1, r, :]
-                    + SIGMA * (up_y(b, bar[0, z + 1, rows(b, 1), :] - u) - v[1]),
-                    pp[2, z + 1, r, :] + (z_up * (bar[0, z + 2, r, :] - u) - SIGMA * v[2]),
-                ]
+                t = [pp[k, z + 1, r, :] for k in range(3)]
+                t[0] = t[0] + SIGMA * halo_next_x(got_u[here, :], 0, z)
+                if b == blocks - 1:
+                    t[1] = t[1] + SIGMA * halo_next_y(bar, 0, z, b)
+                t[2] = t[2] + z_end * bar[0, z + 2, r, :]
                 size = t[0] * t[0] + t[1] * t[1] + t[2] * t[2]
                 scale = jnp.minimum(1.0, ALPHA1 * lax.rsqrt(size))
                 t = [scale * part for part in t]
@@ -275,21 +330,21 @@
                     later.append((p_out, (k, z, here), t[k]))
                 of_p[b] = pack_last(of_p[b], t[0], 0, z)
 
-                half_lo_x = (0.5 * SIGMA) * lo_x
                 received = got_v[here, :]
-                dx = [half_lo_x * (v[k] - prev_x(v[k], received, k, z)) for k in range(3)]
-                dy = [
-                    lo_y(b, (0.5 * SIGMA) * (v[k] - bar[1 + k, z + 1, rows(b, -1), :]))
-                    for k in range(3)
-                ]
-                dz = [z_lo * (v[k] - bar[1 + k, z, r, :]) for k in range(3)]
-                s = [None] * 6
-                s[XX] = qq[XX, z + 1, r, :] + 2.0 * dx[0]
-                s[YY] = qq[YY, z + 1, r, :] + 2.0 * dy[1]
-                s[ZZ] = qq[ZZ, z + 1, r, :] + 2.0 * dz[2]
-                s[XY] = qq[XY, z + 1, r, :] + (dy[0] + dx[1])
-                s[XZ] = qq[XZ, z + 1, r, :] + (dz[0] + dx[2])
-                s[YZ] = qq[YZ, z + 1, r, :] + (dz[1] + dy[2])
+                hx = [halo_prev_x(received, k, z) for k in range(3)]
+                hz = [z_begin * bar[1 + k, z, r, :] for k in range(3)]
+                s = [qq[k, z + 1, r, :] for k in range(6)]
+                s[XX] = s[XX] - SIGMA * hx[0]
+                s[ZZ] = s[ZZ] - SIGMA * hz[2]
+                s[XZ] = s[XZ] - half * (hz[0] + hx[2])
+                if b == 0:
+                    hy = [halo_prev_y(bar, 1 + k, z, b) for k in range(3)]
+                    s[YY] = s[YY] - SIGMA * hy[1]
+                    s[XY] = s[XY] - half * (hy[0] + hx[1])
+                    s[YZ] = s[YZ] - half * (hz[1] + hy[2])
+                else:
+                    s[XY] = s[XY] - half * hx[1]
+                    s[YZ] = s[YZ] - half * hz[1]
                 size = (s[XX] * s[XX] + s[YY] * s[YY] + s[ZZ] * s[ZZ]) + 2.0 * (
                     s[XY] * s[XY] + s[XZ] * s[XZ] + s[YZ] * s[YZ]
                 )
@@ -306,38 +361,57 @@
         store_packed(send_p, of_p)
         store_packed(send_q, of_q)
         start(dual_moves[2:])
-        finish(dual_moves)
-
-        def primal(z, of_u, of_v):
+
+        parts_of = ((XX, XY, XZ), (XY, YY, YZ), (XZ, YZ, ZZ))
+
+        def primal_inside(z):
+            later = []
             z_up, z_lo = up_z(z), lo_z(z)
-            later = []
             for b in range(blocks):
-                if b % GROUP == 0:
-                    flush(later)
                 r, here = rows(b), pl.ds(8 * b, 8)
                 p = [pp[k, z + 1, r, :] for k in range(3)]
                 div = (
-                    (up_x * p[0] - prev_x(p[0], got_p[here, :], 0, z))
-                    + (up_y(b, p[1]) - pp[1, z + 1, rows(b, -1), :])
-                    + (z_up * p[2] - pp[2, z, r, :])
+                    (up_x * p[0] - prev_x(p[0]))
+                    + (up_y(b, p[1]) - prev_y(pp, 1, z, b, p[1]))
+                    + (z_up * p[2] - prev_z(pp, 2, z, b))
                 )
+                new = (u_out[z, here, :] + TAU * div) * gain[z, here, :] + offset[z, here, :]
+                later.append((partial, (0, z, here), new))
                 q = [qq[k, z + 1, r, :] for k in range(6)]
+                for k, (ax, ay, az) in enumerate(parts_of):
+                    div2 = (
+                        (next_x(q[ax]) - lo_x * q[ax])
+                        + (next_y(qq, ay, z, b, q[ay]) - lo_y(b, q[ay]))
+                        + (next_z(qq, az, z, b) - z_lo * q[az])
+                    )
+                    new = v_out[k, z, here, :] + TAU * (p[k] + div2)
+                    later.append((partial, (1 + k, z, here), new))
+            flush(later)
+
+        each(primal_inside)
+        finish(dual_moves)
+
+        def primal(z, of_u, of_v):
+            later = []
+            z_end, z_begin = factor(z == zs - 1), factor(z == 0)
+            for b in range(blocks):
+                r, here = rows(b), pl.ds(8 * b, 8)
                 received = got_q[here, :]
-                new_v = []
-                for k, (ax, ay, az) in enumerate(((XX, XY, XZ), (XY, YY, YZ), (XZ, YZ, ZZ))):
-                    div2 = (
-                        (next_x(q[ax], received, k, z) - lo_x * q[ax])
-                        + (qq[ay, z + 1, rows(b, 1), :] - lo_y(b, q[ay]))
-                        + (qq[az, z + 2, r, :] - z_lo * q[az])
-                    )
+                for k, (ax, ay, az) in enumerate(parts_of):
+                    halo = halo_next_x(received, k, z) + z_end * qq[az, z + 2, r, :]
+                    if b == blocks - 1:
+                        halo = halo + halo_next_y(qq, ay, z, b)
                     old = v_out[k, z, here, :]
-                    new = old + TAU * (p[k] + div2)
+                    new = partial[1 + k, z, here, :] + TAU * halo
                     later.append((v_out, (k, z, here), new))
                     ahead = 2.0 * new - old
                     later.append((bar, (1 + k, z + 1, r), ahead))
                     of_v[b] = pack_last(of_v[b], ahead, k, z)
+                halo = halo_prev_x(got_p[here, :], 0, z) + z_begin * pp[2, z, r, :]
+                if b == 0:
+                    halo = halo + halo_prev_y(pp, 1, z, b)
                 old = u_out[z, here, :]
-                new = (old + TAU * div) * gain[z, here, :] + offset[z, here, :]
+                new = partial[0, z, here, :] - (TAU * halo) * gain[z, here, :]
                 later.append((u_out, (z, here), new))
                 ahead = 2.0 * new - old
                 later.append((bar, (0, z + 1, r), ahead))
@@ -383,6 +457,7 @@
             pltpu.VMEM((6,) + padded, f32),
             pltpu.VMEM((zs, ys, xs), f32),
             pltpu.VMEM((zs, ys, xs), f32),
+            pltpu.VMEM((4, zs, ys, xs), f32),
         ]
         + [face] * 8
         + [

time: 28.9 us -> 28.4 us (0.983)
  Pallas kernels: 28.1 us -> 27.6 us
    pallas_call x1, Pallas kernels: 26.9 us -> 26.4 us  [per_device(): pl.pallas_call(kernel, out_shape=tuple((pltpu.VMEM(a.shape, f32) for a in...]
where the time goes in v3:
time: 28.4 us; the launch traced here: 28.2 us
  Pallas kernels  27.6 us (97%)
  between operations  0.64 us (2%)
    pallas_call x1, Pallas kernels, per_device(): pl.pallas_call(kernel, out_shape=tuple((pltpu.VMEM(a.shape, f32) for a in...  26.4 us
    pallas_call x1, Pallas kernels, per_device(): pl.pallas_call(copy_out, out_shape=tuple((jax.ShapeDtypeStruct(a.shape, f...  1.21 us

profile of v3, /device:TPU:0, one launch (start us, length us, event | category | flops | bytes accessed | tf_op | source)
XLA Modules:
  0.0 28.2 jit_solution(7618399035206685307)
XLA Ops:
  0.6 26.4 %tgv.1 = (f32[8,32,128]{2,1,0:T(8,128)S(1)}, f32[3,8,32,128]{3,2,1,0:T(8,128)S(1)}, f32[3,8,32,128]{3,2,1,0:T(8,128)S(1)}, f32[6,8,32,128]{3,2,1,0:T(8,128)S(1)}) custom-call(f32[8,32,128]{2,1,0:T(8,128)} %noisy_in.1, f32[8,32,128]{2,1,0:T(8,128)} %fid_in.1, f32[8,32,128]{2,1,0:T(8,128)} %u_in.1, f32[3,8,32,128]{3,2,1,0:T(8,128)} %v_in.1, ...), custom_call_target="tpu_custom_call" | custom-call | tf_op jit(solution)/shard_map/tgv/pallas_call | solution.py:449
  27.0 1.2 %out.1 = (f32[8,32,128]{2,1,0:T(8,128)}, f32[3,8,32,128]{3,2,1,0:T(8,128)}, f32[3,8,32,128]{3,2,1,0:T(8,128)}, f32[6,8,32,128]{3,2,1,0:T(8,128)}) custom-call(f32[8,32,128]{2,1,0:T(8,128)S(1)} %get-tuple-element.8.u_in, f32[3,8,32,128]{3,2,1,0:T(8,128)S(1)} %get-tuple-element.9.v_in, f32[3,8,32,128]{3,2,1,0:T(8,128)S(1)} %get-tuple-element.10.p_in, ...), custom_call_target="tpu_custom_call" | custom-call | tf_op jit(solution)/shard_map/out/pallas_call | solution.py:471

commit v4 on v3

--- a/solution.py
+++ b/solution.py
@@ -249,6 +249,8 @@
 
     for load in loads[:2]:
         load.wait()
+    pl.semaphore_wait(barrier, peers)
+    start(primal_moves[:4])
 
     def first_faces(z, packed):
         first, last = list(packed[0]), list(packed[1])
@@ -262,8 +264,7 @@
     first, last = lax.fori_loop(0, zs, first_faces, (nothing, nothing))
     store_packed(send_u, first)
     store_packed(send_v, last)
-    pl.semaphore_wait(barrier, peers)
-    start(primal_moves)
+    start(primal_moves[4:])
 
     for load in loads[2:]:
         load.wait()

time: 28.4 us -> 28.2 us (level)
  no operation moved by 1% of the time
where the time goes in v4:
time: 28.2 us; the launch traced here: 28 us
  Pallas kernels  27.4 us (97%)
  between operations  0.64 us (2%)
    pallas_call x1, Pallas kernels, per_device(): pl.pallas_call(kernel, out_shape=tuple((pltpu.VMEM(a.shape, f32) for a in...  26.2 us
    pallas_call x1, Pallas kernels, per_device(): pl.pallas_call(copy_out, out_shape=tuple((jax.ShapeDtypeStruct(a.shape, f...  1.21 us

profile of v4, /device:TPU:0, one launch (start us, length us, event | category | flops | bytes accessed | tf_op | source)
XLA Modules:
  0.0 28.0 jit_solution(2761717622417301995)
XLA Ops:
  0.6 26.2 %tgv.1 = (f32[8,32,128]{2,1,0:T(8,128)S(1)}, f32[3,8,32,128]{3,2,1,0:T(8,128)S(1)}, f32[3,8,32,128]{3,2,1,0:T(8,128)S(1)}, f32[6,8,32,128]{3,2,1,0:T(8,128)S(1)}) custom-call(f32[8,32,128]{2,1,0:T(8,128)} %noisy_in.1, f32[8,32,128]{2,1,0:T(8,128)} %fid_in.1, f32[8,32,128]{2,1,0:T(8,128)} %u_in.1, f32[3,8,32,128]{3,2,1,0:T(8,128)} %v_in.1, ...), custom_call_target="tpu_custom_call" | custom-call | tf_op jit(solution)/shard_map/tgv/pallas_call | solution.py:450
  26.8 1.2 %out.1 = (f32[8,32,128]{2,1,0:T(8,128)}, f32[3,8,32,128]{3,2,1,0:T(8,128)}, f32[3,8,32,128]{3,2,1,0:T(8,128)}, f32[6,8,32,128]{3,2,1,0:T(8,128)}) custom-call(f32[8,32,128]{2,1,0:T(8,128)S(1)} %get-tuple-element.8.u_in, f32[3,8,32,128]{3,2,1,0:T(8,128)S(1)} %get-tuple-element.9.v_in, f32[3,8,32,128]{3,2,1,0:T(8,128)S(1)} %get-tuple-element.10.p_in, ...), custom_call_target="tpu_custom_call" | custom-call | tf_op jit(solution)/shard_map/out/pallas_call | solution.py:472
